TPU v7x, 512 devices: a whole 4x4x16 slice. The times are simulated.
512 devices in a mesh: freq: 16 (over x, z_lo), line: 32 (over z_hi, y, core).
Axes of the slice: x: 4, y: 4, z: 16 (z_hi: 4, z_lo: 4; z = z_hi * 4 + z_lo), core: 2. Of those that a mesh axis runs over, the one named last changes fastest.
Arguments:
- field: float32 [16, 2, 4, 96, 64, 256], P('freq', None, None, None, 'line'), may hold values from -6 to 6
- live_count: int32 [64], P('line'), may hold values from 64 to 256
- line_owner: int32 [64], replicated, may hold values from 0 to 63, each once
- decomposer: float32 [16, 2, 4, 4, 64, 256], P('freq', None, None, None, 'line'), may hold values from -1.4 to 2.4
- reflection: bfloat16 [16, 1024, 2, 16384], P('freq', None, None, 'line'), may hold values from -0.0625 to 0.0625
- direct_wave: float32 [1024, 16, 2, 384], P('line', 'freq'), may hold values from -6 to 6
Outputs:
- focusing: float32 [1024, 16, 2, 384], P('line', 'freq')
- trace_energy: float32 [1024], P('line')
Inputs may be any that keep to these rules, and one draw needn't show every extreme that they name: `line_owner`: each crossline position appears once.
All inputs are finite; a program needn't handle non-finite values.
Results may differ from a plain program's by a relative error of at most 0.0023.
Values may be sent and summed in bfloat16 or wider, within the bound.
No kernel may reach another device: no remote copies, remote signals or barrier semaphores. Data moves between devices by JAX's collectives and lax.ppermute only.
A program may use at most 64 MiB of HBM per device.

v0:
```python
import math
import jax
import jax.numpy as jnp
from jax import lax
from jax.sharding import Mesh
from jax.sharding import PartitionSpec as P

LINE = ("line_0", "line_1", "line_2")


def in_blocks(shard, dim, count):
    before, after = (shard.shape[:dim], shard.shape[dim + 1 :])
    return jnp.moveaxis(shard.reshape(*before, count, -1, *after), dim, 0)


def scatter_pairs(shard, chips, core, dim):
    sizes = (lax.axis_size(chips), lax.axis_size(core))
    blocks = in_blocks(shard, dim, sizes[0] * sizes[1])
    inside = blocks.shape[1:]
    blocks = blocks.reshape(*sizes, *inside).swapaxes(0, 1).reshape(-1, *inside)
    blocks = lax.psum_scatter(blocks, core, scatter_dimension=0, tiled=True)
    return lax.psum_scatter(blocks, chips, scatter_dimension=0, tiled=True)[0]


def sent_to_all(shard, axis):
    count = lax.axis_size(axis)
    return lax.all_to_all(
        jnp.broadcast_to(shard[None], (count, *shard.shape)), axis, 0, 0, tiled=True
    )


def over_copies(shard, axis):
    return sent_to_all(shard, axis).sum(axis=0)


def phase_tables(line_owner, length):
    wavenum = jnp.arange(length, dtype=jnp.int32)
    products = wavenum[:, None] * line_owner[None, :] % length
    angles = products.astype(jnp.float32) * (2.0 * math.pi / length)
    return (jnp.cos(angles), jnp.sin(angles))


def decompose(operator, spectrum):
    real_rows = []
    imag_rows = []
    for target in range(4):
        real_sum = None
        imag_sum = None
        for source in range(4):
            weight_real = operator[:, 0, target, source][:, None]
            weight_imag = operator[:, 1, target, source][:, None]
            field_real = spectrum[:, 0, source]
            field_imag = spectrum[:, 1, source]
            term_real = weight_real * field_real - weight_imag * field_imag
            term_imag = weight_real * field_imag + weight_imag * field_real
            real_sum = term_real if real_sum is None else real_sum + term_real
            imag_sum = term_imag if imag_sum is None else imag_sum + term_imag
        real_rows.append(real_sum)
        imag_rows.append(imag_sum)
    return jnp.stack([jnp.stack(real_rows, 1), jnp.stack(imag_rows, 1)], 1)


def on_device(field, live_count, line_owner, decomposer, reflection, direct_wave):
    length = line_owner.shape[0]
    receivers = field.shape[5]
    cosine, sine_table = phase_tables(line_owner, length)
    forward_table = jnp.stack([jnp.stack([cosine, sine_table]), jnp.stack([-sine_table, cosine])])
    inverse_table = (
        jnp.stack([jnp.stack([cosine.T, -sine_table.T]), jnp.stack([sine_table.T, cosine.T])])
        / length
    )
    live_mask = jnp.arange(receivers, dtype=jnp.int32)[None, :] < live_count[:, None]
    live_field = jnp.where(live_mask, field, jnp.float32(0.0))
    operator = lax.all_gather(decomposer, LINE, axis=4, tiled=True)
    every_line = lax.all_to_all(live_field, LINE, split_axis=3, concat_axis=4, tiled=True)
    space_all = jnp.einsum(
        "yxjk,fxiokr->fyiojr",
        inverse_table,
        decompose(
            operator,
            jnp.einsum(
                "yxkj,fxiojr->fyiokr", forward_table, every_line, precision=lax.Precision.HIGHEST
            ),
        ),
        precision=lax.Precision.HIGHEST,
    )
    wavefield = lax.all_to_all(
        space_all.astype(jnp.bfloat16), LINE, split_axis=4, concat_axis=3, tiled=True
    )
    freq_count = wavefield.shape[0]
    channels = wavefield.shape[2] * wavefield.shape[3]
    positions = wavefield.shape[4] * wavefield.shape[5]
    wave_bf = wavefield.reshape(freq_count, 2, channels, positions)
    real_part = wave_bf[:, 0]
    imag_part = wave_bf[:, 1]
    stacked = jnp.stack(
        [jnp.stack([real_part, imag_part], 1), jnp.stack([-imag_part, real_part], 1)], 1
    )
    reflected = scatter_pairs(
        jnp.einsum("fsxq,fxocq->sfoc", reflection, stacked, preferred_element_type=jnp.float32),
        ("line_0", "line_1"),
        "line_2",
        0,
    )
    focusing = direct_wave - reflected
    total_freqs = freq_count * lax.axis_size("freq")
    freq_index = lax.axis_index("freq") * freq_count + jnp.arange(freq_count, dtype=jnp.int32)
    weights = 2.0 * (freq_index + 1).astype(jnp.float32) / (total_freqs * (total_freqs + 1))
    partial_value = jnp.sum(jnp.sum(reflected * reflected, axis=(2, 3)) * weights[None, :], axis=1)
    energy_sum = over_copies(partial_value, "freq")
    trace_energy = jnp.sqrt(energy_sum / (2 * channels) + 1e-06)
    return (focusing, trace_energy)


def solution(mesh):
    finer = Mesh(
        mesh.devices.reshape(mesh.shape["freq"], 4, 4, 2), ("freq", "line_0", "line_1", "line_2")
    )
    in_specs = (
        P("freq", None, None, None, LINE, None),
        P(LINE),
        P(),
        P("freq", None, None, None, LINE, None),
        P("freq", None, None, LINE),
        P(LINE, "freq", None, None),
    )
    out_specs = (P(LINE, "freq", None, None), P(LINE))
    return jax.shard_map(
        on_device, mesh=finer, in_specs=in_specs, out_specs=out_specs, check_vma=False
    )
```

profile of v0, /device:TPU:8, one launch (start us, length us, event | category | flops | bytes accessed | tf_op | source)
XLA Modules:
  0.0 385.9 jit_solution(8191804675190697036)
XLA Ops:
  7.2 1.5 copy.86
  8.7 0.7 iota_compare_fusion
  9.4 3.5 copy_select_fusion
  12.9 18.5 %all-to-all-start = ((f32[1,2,4,96,2,256]{5,4,2,1,0,3:T(2,128)}), f32[1,2,4,96,2,256]{5,4,2,1,0,3:T(2,128)S(1)}, u32[]{:S(2)}, u32[]{:S(2)}) async-start(f32[1,2,4,96,2,256]{5,4,2,1,0,3:T(2,128)} %copy_select_fusion), calls=%async_computation | async-start | bytes 3145728 | tf_op jit(solution)/shard_map/all_to_all | solution.py:75
  33.0 100.7 %all-gather.2.cloned.1.call-done = f32[1,2,4,4,64,256]{5,3,2,1,0,4:T(4,128)} async-done(((f32[1,2,4,4,2,256]{5,3,2,1,0,4:T(4,128)}), f32[1,2,4,4,64,256]{5,3,2,1,0,4:T(4,128)}) %all-gather.2.cloned.1.call-update) | async-done | bytes 2097168 | tf_op jit(solution)/shard_map/all_gather | solution.py:74
  133.7 3.3 fusion.51
  137.0 4.3 %fusion.50 = (f32[1,1,1,1,64,256]{5,3,2,1,0,4:T(1,128)S(1)}, f32[1,1,1,1,64,256]{5,3,2,1,0,4:T(1,128)S(1)}, f32[1,1,1,1,64,256]{5,3,2,1,0,4:T(1,128)S(1)}, f32[1...) fusion(f32[1,2,4,4,64,256]{5,3,2,1,0,4:T(4,128)} %all-gather.2., ...), kind=kLoop, calls=%fused_computation.116 | loop fusion | bytes 2490368 | tf_op jit(solution)/shard_map/slice | solution.py:50
  149.9 0.9 copy.201
  150.8 1.1 reshape.1466
  151.9 2.5 fusion.12
  158.5 0.7 copy-done.26
  159.3 1.6 fusion.17
  160.8 0.8 copy.97
  161.6 49.5 %all_to_all.36 = bf16[1,2,4,3,64,256]{5,1,3,2,0,4:T(2,128)(2,1)S(1)} all-to-all(bf16[1,2,4,3,64,256]{5,1,3,2,0,4:T(2,128)(2,1)S(1)} %copy.97), channel_id=1, replica_groups=mesh['freq'=16,'line_0'=4,'line_1'=4,'line_2'=2] {'line_0','line_1','lin..., dimensions={4} | all-to-all | bytes 1572864 | tf_op jit(solution)/shard_map/all_to_all | solution.py:87
  212.9 1.4 copy-done.30
  214.4 3.5 fusion.3
  217.8 2.4 copy.100
  220.2 1.9 copy.101
  222.2 18.9 %reduce-scatter.3.cloned.1.call-done = f32[16,32,1,2,384]{4,1,3,2,0:T(8,128)} async-done(((f32[32,32,1,2,384]{4,1,3,2,0:T(8,128)}), f32[16,32,1,2,384]{4,1,3,2,0:T(8,128)}) %reduce-scatter.3.cloned.1.call-update) | async-done | bytes 1572880 | tf_op jit(solution)/shard_map/reduce_scatter | solution.py:21
  241.1 122.4 %reduce-scatter.5.cloned.1.call-done = f32[1,32,1,2,384]{4,1,3,2,0:T(8,128)} async-done(((f32[16,32,1,2,384]{4,1,3,2,0:T(8,128)}), f32[1,32,1,2,384]{4,1,3,2,0:T(8,128)}) %reduce-scatter.5.cloned.1.call-update) | async-done | bytes 98320 | tf_op jit(solution)/shard_map/reduce_scatter | solution.py:22
  363.5 1.0 fusion.26
  365.1 5.7 %all-to-all-start.2 = ((f32[16,1,32]{2,1,0:T(1,128)}), f32[16,1,32]{2,1,0:T(1,128)S(1)}, u32[]{:S(2)}, u32[]{:S(2)}) async-start(f32[16,1,32]{2,1,0:T(1,128)} %broadcast_in_dim.12), calls=%async_computation.4 | async-start | bytes 16384 | tf_op jit(solution)/shard_map/all_to_all | solution.py:27
  370.9 0.7 copy.104
  371.6 7.2 %all-to-all-done.2 = f32[16,1,32]{2,1,0:T(1,128)S(1)} async-done(((f32[16,1,32]{2,1,0:T(1,128)}), f32[16,1,32]{2,1,0:T(1,128)S(1)}, u32[]{:S(2)}, u32[]{:S(2)}) %all-to-all-start.2) | async-done | bytes 2080 | tf_op jit(solution)/shard_map/all_to_all | solution.py:27
  (105 shorter events, 17.1 us)
Async XLA Ops:
  7.2 126.5 %all-gather.2.cloned.1.call-start = ((), (), s32[]{:S(2)}) async-start(), calls=%async_computation.5 | async-start | bytes 2162688 | tf_op jit(solution)/shard_map/all_gather | solution.py:74
  12.9 18.5 %copy-start.29 = (s32[64]{0:T(128)S(1)}, s32[64]{0:T(128)}, u32[]{:S(2)}) copy-start(s32[64]{0:T(128)} %param.8) | copy-start | bytes 772
  12.9 137.0 %all-to-all-start = ((f32[1,2,4,96,2,256]{5,4,2,1,0,3:T(2,128)}), f32[1,2,4,96,2,256]{5,4,2,1,0,3:T(2,128)S(1)}, u32[]{:S(2)}, u32[]{:S(2)}) async-start(f32[1,2,4,96,2,256]{5,4,2,1,0,3:T(2,128)} %copy_select_fusion), calls=%async_computation | async-start | bytes 3145728 | tf_op jit(solution)/shard_map/all_to_all | solution.py:75
  31.4 209.7 %reduce-scatter.3.cloned.1.call-start = ((), (), s32[]{:S(2)}) async-start(), calls=%async_computation.6 | async-start | bytes 4718592 | tf_op jit(solution)/shard_map/reduce_scatter | solution.py:21
  151.9 2.5 copy-start.2
  151.9 2.5 copy-start.3
  154.6 0.9 copy-start.5
  154.6 0.9 copy-start.6
  154.6 1.0 copy-start.7
  154.6 1.0 copy-start.10
  154.6 1.0 copy-start.11
  155.8 0.9 copy-start.13
  155.8 0.9 copy-start.14
  155.8 1.0 copy-start.15
  155.8 1.0 copy-start.18
  155.9 1.0 copy-start.19
  157.0 0.9 copy-start.22
  157.1 1.0 copy-start.23
  157.1 1.0 copy-start.24
  157.1 1.0 copy-start.25
  212.8 1.6 copy-start.30
  222.1 141.4 %copy-start.28 = (f32[32,1,2,384]{3,2,1,0:T(2,128)S(1)}, f32[32,1,2,384]{3,2,1,0:T(2,128)}, u32[]{:S(2)}) copy-start(f32[32,1,2,384]{3,2,1,0:T(2,128)} %param.11) | copy-start | bytes 294916
  222.2 141.3 %reduce-scatter.5.cloned.1.call-start = ((), (), s32[]{:S(2)}) async-start(), calls=%async_computation.7 | async-start | bytes 1671168 | tf_op jit(solution)/shard_map/reduce_scatter | solution.py:22
  365.1 13.7 %all-to-all-start.2 = ((f32[16,1,32]{2,1,0:T(1,128)}), f32[16,1,32]{2,1,0:T(1,128)S(1)}, u32[]{:S(2)}, u32[]{:S(2)}) async-start(f32[16,1,32]{2,1,0:T(1,128)} %broadcast_in_dim.12), calls=%async_computation.4 | async-start | bytes 16384 | tf_op jit(solution)/shard_map/all_to_all | solution.py:27
  (12 other events, 10.4 us)
Sparse Core Ops, SparseCore 0:
  11.1 122.5 all-gather.1
  222.3 18.7 reduce-scatter.2
  245.2 118.2 reduce-scatter.4
where the time goes:
time: 387 us; the launch traced here: 386 us
  waiting for transfers between devices  249 us (64%)
  blocking collectives  49.5 us (13%)
  local copies, waits for them, and re-layouts  32.4 us (8%)
  starting transfers between devices  24.3 us (6%)
  between operations  14.2 us (4%)
  other arithmetic  8.75 us (2%)
  matrix products  7.49 us (2%)
    reduce_scatter x1, waiting for transfers between devices, scatter_pairs(): return lax.psum_scatter(blocks, chips, scatter_dimension=0, tiled=True)[0]  122 us
    all_gather x1, waiting for transfers between devices, on_device(): operator = lax.all_gather(decomposer, LINE, axis=4, tiled=True)  101 us
    all_to_all x1, blocking collectives, on_device(): lax.all_to_all(space_all.astype(jnp.bfloat16), LINE, split_axis=4, concat...  49.5 us
    reduce_scatter x1, waiting for transfers between devices, scatter_pairs(): blocks = lax.psum_scatter(blocks, core, scatter_dimension=0, tiled=True)  18.9 us
    all_to_all x1, starting transfers between devices, on_device(): lax.all_to_all(live_field, LINE, split_axis=3, concat_axis=4, tiled=True)  18.5 us
    unnamed x80, local copies, waits for them, and re-layouts  15.5 us
  transfers between devices with their start and end apart: 5, of which 4 were waited for; matrix products, arithmetic and copies ran while one was open for 6% of the time, Pallas kernels for 0%

commit v1 on v0

--- a/solution.py
+++ b/solution.py
@@ -71,7 +71,9 @@
     )
     live_mask = jnp.arange(receivers, dtype=jnp.int32)[None, :] < live_count[:, None]
     live_field = jnp.where(live_mask, field, jnp.float32(0.0))
-    operator = lax.all_gather(decomposer, LINE, axis=4, tiled=True)
+    operator = jnp.concatenate(
+        lax.all_to_all(jnp.stack([decomposer] * lax.axis_size(LINE)), LINE, 0, 0), axis=4
+    )
     every_line = lax.all_to_all(live_field, LINE, split_axis=3, concat_axis=4, tiled=True)
     space_all = jnp.einsum(
         "yxjk,fxiokr->fyiojr",

time: 387 us -> 444 us (1.15)
  blocking collectives: 49.5 us -> 144 us
  local copies, waits for them, and re-layouts: 32.4 us -> 20.2 us
  starting transfers between devices: 24.3 us -> 12.4 us
  waiting for transfers between devices: 249 us -> 239 us
    all_gather x1 -> x0, waiting for transfers between devices: 101 us -> none  [on_device(): operator = lax.all_gather(decomposer, LINE, axis=4, tiled=True)]
    all_to_all x0 -> x1, blocking collectives: none -> 95.7 us  [on_device(): lax.all_to_all(live_field, LINE, split_axis=3, concat_axis=4, tiled=True)]
    all_to_all x1, waiting for transfers between devices: 0.01 us -> 92.7 us  [on_device(): lax.all_to_all(jnp.stack([decomposer] * lax.axis_size(LINE)), LINE, 0, 0)]
    unnamed x80 -> x25, local copies, waits for them, and re-layouts: 15.5 us -> 2.36 us
    all_to_all x1, starting transfers between devices: 18.5 us -> 6.47 us  [on_device(): lax.all_to_all(jnp.stack([decomposer] * lax.axis_size(LINE)), LINE, 0, 0)]
  transfers between devices with their start and end apart: 5 -> 4, of which waited for: 4 -> 4; matrix products, arithmetic and copies ran while one was open for 6% -> 2% of each run, Pallas kernels for 0% -> 0%
where the time goes in v1:
time: 444 us; the launch traced here: 443 us
  waiting for transfers between devices  239 us (54%)
  blocking collectives  144 us (32%)
  local copies, waits for them, and re-layouts  20.2 us (5%)
  between operations  14.4 us (3%)
  starting transfers between devices  12.4 us (3%)
  matrix products  6.58 us (1%)
  other arithmetic  6.33 us (1%)
    reduce_scatter x1, waiting for transfers between devices, scatter_pairs(): return lax.psum_scatter(blocks, chips, scatter_dimension=0, tiled=True)[0]  123 us
    all_to_all x1, blocking collectives, on_device(): lax.all_to_all(live_field, LINE, split_axis=3, concat_axis=4, tiled=True)  95.7 us
    all_to_all x1, waiting for transfers between devices, on_device(): lax.all_to_all(jnp.stack([decomposer] * lax.axis_size(LINE)), LINE, 0, 0)  92.7 us
    all_to_all x1, blocking collectives, on_device(): lax.all_to_all(space_all.astype(jnp.bfloat16), LINE, split_axis=4, concat...  48.8 us
    reduce_scatter x1, waiting for transfers between devices, scatter_pairs(): blocks = lax.psum_scatter(blocks, core, scatter_dimension=0, tiled=True)  16.1 us
  transfers between devices with their start and end apart: 4, of which 4 were waited for; matrix products, arithmetic and copies ran while one was open for 2% of the time, Pallas kernels for 0%

profile of v1, /device:TPU:8, one launch (start us, length us, event | category | flops | bytes accessed | tf_op | source)
XLA Modules:
  0.0 443.2 jit_solution(11182954298783934100)
XLA Ops:
  7.2 0.7 iota_compare_fusion
  7.9 2.3 copy_select_fusion
  10.2 95.7 %all_to_all.41 = f32[1,2,4,96,2,256]{5,4,2,1,0,3:T(2,128)S(1)} all-to-all(f32[1,2,4,96,2,256]{5,4,2,1,0,3:T(2,128)S(1)} %copy_select_fusion), channel_id=1, replica_groups=mesh['freq'=16,'line_0'=4,'line_1'=4,'line_2'=2] {'line_0','line_1','lin..., dimensions={3} | all-to-all | bytes 3145728 | tf_op jit(solution)/shard_map/all_to_all | solution.py:77
  105.9 2.3 stack.40
  108.2 6.5 %all-to-all-start = ((f32[32,1,2,4,4,2,256]{6,5,4,3,2,1,0:T(2,128)}), f32[32,1,2,4,4,2,256]{6,5,4,3,2,1,0:T(2,128)}, u32[]{:S(2)}, u32[]{:S(2)}) async-start(f32[32,1,2,4,4,2,256]{6,5,4,3,2,1,0:T(2,128)} %stack.40), calls=%async_computation | async-start | bytes 4194304 | tf_op jit(solution)/shard_map/all_to_all | solution.py:75
  115.3 2.0 copy.218
  117.3 2.4 reshape.1477
  119.7 1.6 fusion.12
  121.2 92.7 %all-to-all-done = f32[32,1,2,4,4,2,256]{6,5,4,3,2,1,0:T(2,128)} async-done(((f32[32,1,2,4,4,2,256]{6,5,4,3,2,1,0:T(2,128)}), f32[32,1,2,4,4,2,256]{6,5,4,3,2,1,0:T(2,128)}, u32[]{:S(2)}, u32[]{:S(2)}) %all-to-all-start) | async-done | bytes 2097184 | tf_op jit(solution)/shard_map/all_to_all | solution.py:75
  213.9 2.1 copy.103
  216.1 1.0 fusion.50
  219.4 1.6 fusion.17
  221.0 0.8 copy.114
  221.8 48.8 %all_to_all.42 = bf16[1,2,4,3,64,256]{5,1,3,2,0,4:T(2,128)(2,1)S(1)} all-to-all(bf16[1,2,4,3,64,256]{5,1,3,2,0,4:T(2,128)(2,1)S(1)} %copy.114), channel_id=1, replica_groups=mesh['freq'=16,'line_0'=4,'line_1'=4,'line_2'=2] {'line_0','line_1','lin..., dimensions={4} | all-to-all | bytes 1572864 | tf_op jit(solution)/shard_map/all_to_all | solution.py:89
  272.4 1.4 copy-done.3
  273.9 3.5 fusion.3
  277.3 2.4 copy.117
  279.7 1.9 copy.118
  281.7 16.1 %reduce-scatter.3.cloned.1.call-done = f32[16,32,1,2,384]{4,1,3,2,0:T(8,128)} async-done(((f32[32,32,1,2,384]{4,1,3,2,0:T(8,128)}), f32[16,32,1,2,384]{4,1,3,2,0:T(8,128)}) %reduce-scatter.3.cloned.1.call-update) | async-done | bytes 1572880 | tf_op jit(solution)/shard_map/reduce_scatter | solution.py:21
  297.8 122.7 %reduce-scatter.5.cloned.1.call-done = f32[1,32,1,2,384]{4,1,3,2,0:T(8,128)} async-done(((f32[16,32,1,2,384]{4,1,3,2,0:T(8,128)}), f32[1,32,1,2,384]{4,1,3,2,0:T(8,128)}) %reduce-scatter.5.cloned.1.call-update) | async-done | bytes 98320 | tf_op jit(solution)/shard_map/reduce_scatter | solution.py:22
  420.6 1.0 fusion.26
  422.2 5.7 %all-to-all-start.3 = ((f32[16,1,32]{2,1,0:T(1,128)}), f32[16,1,32]{2,1,0:T(1,128)S(1)}, u32[]{:S(2)}, u32[]{:S(2)}) async-start(f32[16,1,32]{2,1,0:T(1,128)} %broadcast_in_dim.12), calls=%async_computation.5 | async-start | bytes 16384 | tf_op jit(solution)/shard_map/all_to_all | solution.py:27
  427.9 0.7 copy.121
  428.6 7.2 %all-to-all-done.3 = f32[16,1,32]{2,1,0:T(1,128)S(1)} async-done(((f32[16,1,32]{2,1,0:T(1,128)}), f32[16,1,32]{2,1,0:T(1,128)S(1)}, u32[]{:S(2)}, u32[]{:S(2)}) %all-to-all-start.3) | async-done | bytes 2080 | tf_op jit(solution)/shard_map/all_to_all | solution.py:27
  (50 shorter events, 5.7 us)
Async XLA Ops:
  10.2 95.7 %copy-start.1 = (f32[1,2,4,4,2,256]{5,4,3,2,1,0:T(2,128)S(1)}, f32[1,2,4,4,2,256]{5,4,3,2,1,0:T(2,128)}, u32[]{:S(2)}) copy-start(f32[1,2,4,4,2,256]{5,4,3,2,1,0:T(2,128)} %param.9) | copy-start | bytes 196612
  108.2 6.7 %copy-start.2 = (s32[64]{0:T(128)S(1)}, s32[64]{0:T(128)}, u32[]{:S(2)}) copy-start(s32[64]{0:T(128)} %param.8) | copy-start | bytes 772
  108.2 105.7 %all-to-all-start = ((f32[32,1,2,4,4,2,256]{6,5,4,3,2,1,0:T(2,128)}), f32[32,1,2,4,4,2,256]{6,5,4,3,2,1,0:T(2,128)}, u32[]{:S(2)}, u32[]{:S(2)}) async-start(f32[32,1,2,4,4,2,256]{6,5,4,3,2,1,0:T(2,128)} %stack.40), calls=%async_computation | async-start | bytes 4194304 | tf_op jit(solution)/shard_map/all_to_all | solution.py:75
  114.7 183.1 %reduce-scatter.3.cloned.1.call-start = ((), (), s32[]{:S(2)}) async-start(), calls=%async_computation.6 | async-start | bytes 4718592 | tf_op jit(solution)/shard_map/reduce_scatter | solution.py:21
  272.3 1.6 copy-start.3
  281.6 138.9 %copy-start = (f32[32,1,2,384]{3,2,1,0:T(2,128)S(1)}, f32[32,1,2,384]{3,2,1,0:T(2,128)}, u32[]{:S(2)}) copy-start(f32[32,1,2,384]{3,2,1,0:T(2,128)} %param.11) | copy-start | bytes 294916
  281.7 138.9 %reduce-scatter.5.cloned.1.call-start = ((), (), s32[]{:S(2)}) async-start(), calls=%async_computation.7 | async-start | bytes 1671168 | tf_op jit(solution)/shard_map/reduce_scatter | solution.py:22
  422.2 13.6 %all-to-all-start.3 = ((f32[16,1,32]{2,1,0:T(1,128)}), f32[16,1,32]{2,1,0:T(1,128)S(1)}, u32[]{:S(2)}, u32[]{:S(2)}) async-start(f32[16,1,32]{2,1,0:T(1,128)} %broadcast_in_dim.12), calls=%async_computation.5 | async-start | bytes 16384 | tf_op jit(solution)/shard_map/all_to_all | solution.py:27
Sparse Core Ops, SparseCore 0:
  281.8 15.9 reduce-scatter.2
  301.9 118.6 reduce-scatter.4
